TPU v7x, 32 devices: a whole 2x2x4 slice. The times are simulated.
32 devices in a mesh: seq: 8 (over z, y), tp: 4 (over x, core).
Axes of the slice: x: 2, y: 2, z: 4, core: 2. Of those that a mesh axis runs over, the one named last changes fastest.
Arguments:
- latents: bfloat16 [1024, 3072], P('seq', 'tp'), may hold values from -6 to 6
- lengths: int32 [2], replicated, may hold values from 1 to 768, 1024 in all
- t_index: int32 [2], replicated, may hold values from 0 to 6
- mod_scale: float32 [3072], replicated, may hold values from -2 to 2
- q_weight: bfloat16 [3072, 2048], P(None, 'tp'), may hold values from -0.109375 to 0.109375
- k_weight: bfloat16 [3072, 2048], P(None, 'tp'), may hold values from -0.109375 to 0.109375
- v_weight: bfloat16 [3072, 2048], P(None, 'tp'), may hold values from -0.109375 to 0.109375
- out_weight: bfloat16 [2048, 3072], P('tp'), may hold values from -0.1875 to 0.1875
- q_gain: float32 [128], replicated, may hold values from 0.6 to 2.4
- k_gain: float32 [128], replicated, may hold values from 0.6 to 2.4
- student_weight: bfloat16 [3072, 3072], P('tp'), may hold values from -0.15625 to 0.15625
Outputs:
- target: bfloat16 [1024, 3072], P('seq', 'tp')
- student_velocity: bfloat16 [1024, 3072], P('seq', 'tp')
- loss: float32 [], replicated
Inputs may be any that keep to these rules, and one draw needn't show every extreme that they name: lengths sum to 1024.
All inputs are finite; a program needn't handle non-finite values.
Results may differ from a plain program's by a relative error of at most 0.024.
Values may be sent and summed in bfloat16 or wider, within the bound.
No kernel may reach another device: no remote copies, remote signals or barrier semaphores. Data moves between devices by JAX's collectives and lax.ppermute only.
A program may use at most 64 MiB of HBM per device.

v0:
```python
import math
import jax
import jax.numpy as jnp
from jax import lax
from jax.sharding import PartitionSpec as P

TGRID = 8
epsilon = 1e-06
kinetic_weight = 0.1


def image_index(positions, image_ends):
    return jnp.sum((positions[:, None] >= image_ends[None, :]).astype(jnp.int32), axis=1)


def head_norm(projected, gain):
    shaped = projected.reshape(projected.shape[0], -1, gain.shape[0])
    normed = shaped * lax.rsqrt(jnp.mean(shaped * shaped, axis=-1, keepdims=True) + epsilon) * gain
    return normed.astype(jnp.bfloat16)


def teacher(
    state, times, query_image, image_ends, mod_scale, q_weight, k_weight, v_weight, q_gain, k_gain
):
    row_count = state.shape[0]
    head_dim = q_gain.shape[0]
    state32 = state.astype(jnp.float32)
    normed = state32 * lax.rsqrt(jnp.mean(state32 * state32, axis=1, keepdims=True) + epsilon)
    hidden = (normed * (1.0 + times[:, None] * mod_scale[None, :])).astype(jnp.bfloat16)
    queries = head_norm(jnp.dot(hidden, q_weight, preferred_element_type=jnp.float32), q_gain)
    key_rows = head_norm(jnp.dot(hidden, k_weight, preferred_element_type=jnp.float32), k_gain)
    key_rows = key_rows.reshape(row_count, -1)
    value_rows = jnp.dot(hidden, v_weight, preferred_element_type=jnp.float32).astype(jnp.bfloat16)
    heads_here = queries.shape[1]
    score_scale = 1.0 / math.sqrt(head_dim)

    def attend(carry, key_block, value_block):
        running_max, running_total, running_sum = carry
        count = key_block.shape[0]
        key_image = image_index(jnp.arange(count, dtype=jnp.int32), image_ends)
        key_heads = key_block.reshape(count, heads_here, head_dim)
        value_heads = value_block.reshape(count, heads_here, head_dim)
        same_image = (query_image[:, None] == key_image[None, :])[:, None, :]
        scores = (
            jnp.einsum("qhd,khd->qhk", queries, key_heads, preferred_element_type=jnp.float32)
            * score_scale
        )
        scores = jnp.where(same_image, scores, -1e30)
        new_max = jnp.maximum(running_max, jnp.max(scores, axis=2))
        weights = jnp.where(same_image, jnp.exp(scores - new_max[:, :, None]), 0.0)
        new_total = jnp.sum(weights, axis=2)
        product = jnp.einsum(
            "qhk,khd->qhd",
            weights.astype(jnp.bfloat16),
            value_heads,
            preferred_element_type=jnp.float32,
        )
        return (new_max, new_total, product)

    start_carry = (
        jnp.full((row_count, heads_here), -1e30, jnp.float32),
        jnp.zeros((row_count, heads_here), jnp.float32),
        jnp.zeros((row_count, heads_here, head_dim), jnp.float32),
    )
    offset = jnp.int32(0)
    key_block = lax.all_gather(key_rows, "seq", axis=0, tiled=True)
    value_block = lax.all_gather(value_rows, "seq", axis=0, tiled=True)
    count = key_block.shape[0]
    first_image = image_index(jnp.reshape(offset, (1,)), image_ends)[0]
    last_image = image_index(jnp.reshape(offset + count - 1, (1,)), image_ends)[0]
    touches = jnp.logical_and(first_image <= query_image[-1], last_image >= query_image[0])
    final_max, final_total, final_sum = lax.cond(
        touches,
        lambda inner: attend(inner, key_block, value_block),
        lambda inner: inner,
        start_carry,
    )
    mixed = (final_sum / final_total[:, :, None]).astype(jnp.bfloat16).reshape(row_count, -1)
    return (mixed, hidden)


def on_device(
    latents,
    lengths,
    t_index,
    mod_scale,
    q_weight,
    k_weight,
    v_weight,
    out_weight,
    q_gain,
    k_gain,
    student_weight,
):
    row_count, width_here = latents.shape
    tp_index = lax.axis_index("tp")
    image_ends = jnp.cumsum(lengths)
    row_offset = lax.axis_index("seq") * row_count
    query_image = image_index(row_offset + jnp.arange(row_count, dtype=jnp.int32), image_ends)
    one_hot = (
        query_image[:, None] == jnp.arange(lengths.shape[0], dtype=jnp.int32)[None, :]
    ).astype(jnp.float32)
    start_times = jnp.sum(one_hot * (t_index.astype(jnp.float32) / TGRID)[None, :], axis=1)
    step_size = 1.0 / TGRID
    whole_rows = lax.all_gather(latents, "tp", axis=1, tiled=True)
    velocities = []
    first_hidden = whole_rows
    state_shard = latents
    for euler_index in range(2):
        if euler_index == 1:
            whole_rows = lax.all_gather(state_shard, "tp", axis=1, tiled=True)
        mixed, hidden = teacher(
            whole_rows,
            start_times + euler_index * step_size,
            query_image,
            image_ends,
            mod_scale,
            q_weight,
            k_weight,
            v_weight,
            q_gain,
            k_gain,
        )
        if euler_index == 0:
            first_hidden = hidden
        partial_value = jnp.dot(mixed, out_weight, preferred_element_type=jnp.float32)
        velocity = lax.psum_scatter(
            partial_value.astype(jnp.bfloat16), "tp", scatter_dimension=1, tiled=True
        )
        velocities.append(velocity)
        state_shard = (
            latents.astype(jnp.float32) + step_size * velocity.astype(jnp.float32)
        ).astype(jnp.bfloat16)
    columns = lax.dynamic_slice_in_dim(first_hidden, tp_index * width_here, width_here, 1)
    student_terms = jnp.dot(columns, student_weight, preferred_element_type=jnp.float32)
    student_velocity = lax.psum_scatter(
        student_terms.astype(jnp.bfloat16), "tp", scatter_dimension=1, tiled=True
    )
    target = (0.5 * (velocities[0].astype(jnp.float32) + velocities[1].astype(jnp.float32))).astype(
        jnp.bfloat16
    )
    student32 = student_velocity.astype(jnp.float32)
    residual = student32 - target.astype(jnp.float32)
    per_token = jnp.sum(residual * residual, axis=1) + kinetic_weight * jnp.sum(
        student32 * student32, axis=1
    )
    image_part = jnp.sum(one_hot * per_token[:, None], axis=0)
    image_sum = lax.psum(image_part, ("seq", "tp"))
    loss = jnp.mean(image_sum / (lengths.astype(jnp.float32) * mod_scale.shape[0]))
    return (target, student_velocity, loss)


def solution(mesh):
    placed = (
        P("seq", "tp"),
        P(),
        P(),
        P(),
        P(None, "tp"),
        P(None, "tp"),
        P(None, "tp"),
        P("tp", None),
        P(),
        P(),
        P("tp", None),
    )
    return jax.shard_map(
        on_device,
        mesh=mesh,
        in_specs=placed,
        out_specs=(P("seq", "tp"), P("seq", "tp"), P()),
        check_vma=False,
    )
```

profile of v0, /device:TPU:0, one launch (start us, length us, event | category | flops | bytes accessed | tf_op | source)
XLA Modules:
  0.0 336.3 jit_solution(12734759485271382639)
XLA Ops:
  8.1 10.4 %all_gather.18 = bf16[128,3072]{1,0:T(8,128)(2,1)S(1)} all-gather(bf16[128,768]{1,0:T(8,128)(2,1)} %param.15), channel_id=1, replica_groups=mesh['seq'=8,'tp'=4] {'tp'}, dimensions={1}, use_global_device_ids=true | all-gather | bytes 983040 | tf_op jit(solution)/shard_map/all_gather | solution.py:105
  23.6 3.1 convolution_convert_fusion.4
  26.8 3.4 %fusion.70 = (f32[128,512]{1,0:T(8,128)}, f32[128,512]{1,0:T(8,128)S(1)}) fusion(bf16[128,3072]{1,0:T(8,128)(2,1)} %copy-done.1, bf16[3072,512]{1,0:T(8,128)(2,1)} %param.20), kind=kOutput, calls=%fused_computation.115 | convolution fusion | flops 402718720 | bytes 4456448 | tf_op jit(solution)/shard_map/dot_general | solution.py:31
  30.2 1.8 mul.218
  38.0 2.7 fusion.72
  42.9 25.1 %all-gather.7.cloned.1.call-done = bf16[1024,512]{1,0:T(8,128)(2,1)} async-done(((bf16[128,512]{1,0:T(8,128)(2,1)}), bf16[1024,512]{1,0:T(8,128)(2,1)}) %all-gather.7.cloned.1.call-update) | async-done | bytes 1048592 | tf_op jit(solution)/shard_map/all_gather | solution.py:67
  68.0 41.7 %all-gather.5.cloned.1.call-done = bf16[1024,512]{1,0:T(8,128)(2,1)} async-done(((bf16[128,512]{1,0:T(8,128)(2,1)}), bf16[1024,512]{1,0:T(8,128)(2,1)}) %all-gather.5.cloned.1.call-update) | async-done | bytes 1048592 | tf_op jit(solution)/shard_map/all_gather | solution.py:66
  109.7 6.0 %conditional.2 = (f32[128,4]{0,1:T(4,128)S(1)}, f32[128,4,128]{0,2,1:T(8,128)S(1)}) conditional(s32[]{:T(128)} %convert_element_type.124, () %tuple.24, (s32[128]{0:T(128)S(1)}, s32[2]{0:T(128)}, bf16[1024,512]{1,0:T(8,128)(2,1)}, bf16[128,4,128]{2,0,1:T(8,128)(2,1)S(1)}, bf16[1024,512]{1,0:T(8,128)(2,1)}) %tuple.59), branch_computations={%region_8.9_spmd, %region_9.13_spmd} | conditional | flops 275386880 | bytes 14045748 | solution.py:72
  110.7 1.7 fusion
  117.4 22.0 %reduce-scatter.4.cloned.1.call-done = bf16[128,768]{1,0:T(8,128)(2,1)} async-done(((bf16[128,3072]{1,0:T(8,128)(2,1)}), bf16[128,768]{1,0:T(8,128)(2,1)}) %reduce-scatter.4.cloned.1.call-update) | async-done | bytes 196624 | tf_op jit(solution)/shard_map/reduce_scatter | solution.py:127
  140.4 8.0 %all_gather.21 = bf16[128,3072]{1,0:T(8,128)(2,1)S(1)} all-gather(bf16[128,768]{1,0:T(8,128)(2,1)S(1)} %fusion.43), channel_id=1, replica_groups=mesh['seq'=8,'tp'=4] {'tp'}, dimensions={1}, use_global_device_ids=true | all-gather | bytes 983040 | tf_op jit(solution)/shard_map/all_gather | solution.py:111
  149.3 3.2 convolution_convert_fusion.3
  152.6 3.6 %fusion.71 = (f32[128,512]{1,0:T(8,128)}, f32[128,512]{1,0:T(8,128)}) fusion(bf16[3072,512]{1,0:T(8,128)(2,1)} %param.20, bf16[128,3072]{1,0:T(8,128)(2,1)} %copy-done.3, f32[128]{0:T(128)S(1)} %broadcast_add_fusion, f32[128]{0:T(128)S(1)} %add_rsqrt_fusion.4, f32[3072]{0:T(1024)S(1)} %copy-done.6), kind=kOutput, calls=%fused_computation.116 | convolution fusion | flops 405078016 | bytes 4469760 | tf_op jit(solution)/shard_map/dot_general | solution.py:31
  157.6 1.6 fusion.50
  159.4 4.2 %convolution_convert_fusion.2 = bf16[128,3072]{1,0:T(8,128)(2,1)} fusion(bf16[768,3072]{1,0:T(8,128)(2,1)} %param.25, bf16[128,3072]{1,0:T(8,128)(2,1)} %copy-done.1, s32[]{:T(128)S(6)} %select_n.16), kind=kOutput, calls=%fused_computation.48 | convolution fusion | flops 604372992 | bytes 5701636 | tf_op jit(solution)/shard_map/dot_general | solution.py:135
  163.7 3.5 %fusion.64 = f32[128,512]{1,0:T(8,128)} fusion(bf16[3072,512]{1,0:T(8,128)(2,1)} %param.19, bf16[128,3072]{1,0:T(8,128)(2,1)} %copy-done.3, f32[128]{0:T(128)S(1)} %broadcast_add_fusion, f32[128]{0:T(128)S(1)} %add_rsqrt_fusion.4, f32[3072]{0:T(1024)S(1)} %copy-done.6), kind=kOutput, calls=%fused_computation.112 | convolution fusion | flops 405012480 | bytes 4207616 | tf_op jit(solution)/shard_map/dot_general | solution.py:30
  169.6 23.9 %all-gather.11.cloned.1.call-done = bf16[1024,512]{1,0:T(8,128)(2,1)} async-done(((bf16[128,512]{1,0:T(8,128)(2,1)}), bf16[1024,512]{1,0:T(8,128)(2,1)}) %all-gather.11.cloned.1.call-update) | async-done | bytes 1048592 | tf_op jit(solution)/shard_map/all_gather | solution.py:67
  193.5 41.6 %all-gather.9.cloned.1.call-done = bf16[1024,512]{1,0:T(8,128)(2,1)} async-done(((bf16[128,512]{1,0:T(8,128)(2,1)}), bf16[1024,512]{1,0:T(8,128)(2,1)}) %all-gather.9.cloned.1.call-update) | async-done | bytes 1048592 | tf_op jit(solution)/shard_map/all_gather | solution.py:66
  235.1 5.3 %conditional.3 = (f32[128,4]{0,1:T(4,128)S(1)}, f32[128,4,128]{0,2,1:T(8,128)S(1)}) conditional(s32[]{:T(128)} %convert_element_type.124, () %tuple.26, (s32[128]{0:T(128)S(1)}, s32[2]{0:T(128)S(1)}, bf16[1024,512]{1,0:T(8,128)(2,1)}, bf16[128,4,128]{2,0,1:T(8,128)(2,1)S(1)}, bf16[1024,512]{1,0:T(8,128)(2,1)}) %tuple.60), branch_computations={%region_17.18_spmd, %region_18.0_spmd} | conditional | flops 275386880 | bytes 14045748 | solution.py:72
  235.4 1.8 fusion.18
  242.0 18.1 %reduce-scatter.8.cloned.1.call-done = bf16[128,768]{1,0:T(8,128)(2,1)} async-done(((bf16[128,3072]{1,0:T(8,128)(2,1)}), bf16[128,768]{1,0:T(8,128)(2,1)}) %reduce-scatter.8.cloned.1.call-update) | async-done | bytes 196624 | tf_op jit(solution)/shard_map/reduce_scatter | solution.py:136
  260.0 25.8 %reduce-scatter.6.cloned.1.call-done = bf16[128,768]{1,0:T(8,128)(2,1)} async-done(((bf16[128,3072]{1,0:T(8,128)(2,1)}), bf16[128,768]{1,0:T(8,128)(2,1)}) %reduce-scatter.6.cloned.1.call-update) | async-done | bytes 196624 | tf_op jit(solution)/shard_map/reduce_scatter | solution.py:127
  285.8 1.8 fusion.48
  287.8 39.3 %psum.7 = f32[2]{0:T(128)S(1)} all-reduce(f32[2]{0:T(128)S(1)} %select_reduce_fusion), channel_id=1, replica_groups=mesh['seq'=8,'tp'=4] {'seq','tp'}, use_global_device_ids=true, to_apply=%region_27.28 | all-reduce | flops 2 | bytes 16 | tf_op jit(solution)/shard_map/psum | solution.py:148
  (98 shorter events, 29.2 us)
Async XLA Ops:
  7.2 108.6 %copy-start = (bf16[512,3072]{1,0:T(8,128)(2,1)S(1)}, bf16[512,3072]{1,0:T(8,128)(2,1)}, u32[]{:S(2)}) copy-start(bf16[512,3072]{1,0:T(8,128)(2,1)} %param.22) | copy-start | bytes 9437188
  7.2 60.8 %all-gather.7.cloned.1.call-start = ((), (), s32[]{:S(2)}) async-start(), calls=%async_computation.4 | async-start | bytes 1179648 | tf_op jit(solution)/shard_map/all_gather | solution.py:67
  18.5 0.9 copy-start.2
  20.4 14.4 %copy-start.8 = (s32[2,1]{0,1:T(1,128)}, s32[2,1]{0,1:T(1,128)S(1)}, u32[]{:S(2)}) copy-start(s32[2,1]{0,1:T(1,128)S(1)} %reduce-window.4) | copy-start | bytes 28
  20.6 0.6 copy-start.10
  22.7 0.9 copy-start.1
  26.7 6.4 %copy-start.12 = (f32[128]{0:T(128)S(1)}, f32[128]{0:T(128)}, u32[]{:S(2)}) copy-start(f32[128]{0:T(128)} %param.24) | copy-start | bytes 1540
  26.7 83.0 %all-gather.5.cloned.1.call-start = ((), (), s32[]{:S(2)}) async-start(), calls=%async_computation.3 | async-start | bytes 1179648 | tf_op jit(solution)/shard_map/all_gather | solution.py:66
  34.1 105.3 %reduce-scatter.4.cloned.1.call-start = ((), (), s32[]{:S(2)}) async-start(), calls=%async_computation.5 | async-start | bytes 983040 | tf_op jit(solution)/shard_map/reduce_scatter | solution.py:127
  38.0 4.8 %copy-start.7 = (f32[128]{0:T(128)S(1)}, f32[128]{0:T(128)}, u32[]{:S(2)}) copy-start(f32[128]{0:T(128)} %param.23) | copy-start | bytes 1540
  109.7 2.8 copy-start.14
  115.8 1.6 copy-start.11
  115.8 23.6 %copy-start.5 = (bf16[128,768]{1,0:T(8,128)(2,1)S(1)}, bf16[128,768]{1,0:T(8,128)(2,1)}, u32[]{:S(2)}) copy-start(bf16[128,768]{1,0:T(8,128)(2,1)} %param.15) | copy-start | bytes 589828
  117.3 32.0 %copy-start.6 = (f32[3072]{0:T(1024)S(1)}, f32[3072]{0:T(1024)}, u32[]{:S(2)}) copy-start(f32[3072]{0:T(1024)} %param.18) | copy-start | bytes 36868
  117.3 76.2 %all-gather.11.cloned.1.call-start = ((), (), s32[]{:S(2)}) async-start(), calls=%async_computation.7 | async-start | bytes 1179648 | tf_op jit(solution)/shard_map/all_gather | solution.py:67
  148.4 0.9 copy-start.3
  152.5 82.5 %all-gather.9.cloned.1.call-start = ((), (), s32[]{:S(2)}) async-start(), calls=%async_computation.6 | async-start | bytes 1179648 | tf_op jit(solution)/shard_map/all_gather | solution.py:66
  159.3 100.7 %reduce-scatter.8.cloned.1.call-start = ((), (), s32[]{:S(2)}) async-start(), calls=%async_computation.9 | async-start | bytes 983040 | tf_op jit(solution)/shard_map/reduce_scatter | solution.py:136
  163.6 122.2 %reduce-scatter.6.cloned.1.call-start = ((), (), s32[]{:S(2)}) async-start(), calls=%async_computation.8 | async-start | bytes 983040 | tf_op jit(solution)/shard_map/reduce_scatter | solution.py:127
  163.7 71.4 %copy-start.9 = (s32[2,1]{0,1:T(1,128)S(1)}, s32[2,1]{0,1:T(1,128)}, u32[]{:S(2)}) copy-start(s32[2,1]{0,1:T(1,128)} %copy-done.8) | copy-start | bytes 28
  235.1 2.1 copy-start.13
  240.4 45.4 %copy-start.4 = (bf16[128,768]{1,0:T(8,128)(2,1)S(1)}, bf16[128,768]{1,0:T(8,128)(2,1)}, u32[]{:S(2)}) copy-start(bf16[128,768]{1,0:T(8,128)(2,1)} %reduce-scatter.4.cloned.1.call-done) | copy-start | bytes 589828
  240.4 86.6 %copy-start.15 = (s32[2]{0:T(128)S(1)}, s32[2]{0:T(128)}, u32[]{:S(2)}) copy-start(s32[2]{0:T(128)} %param.16) | copy-start | bytes 28
Sparse Core Ops, SparseCore 0:
  26.8 41.1 all-gather.6
  70.7 38.9 all-gather.4
  117.4 21.9 reduce-scatter.3
  152.6 40.8 all-gather.10
  196.0 38.9 all-gather.8
  238.0 21.9 reduce-scatter.7
  262.5 23.2 reduce-scatter.5
where the time goes:
time: 337 us; the launch traced here: 336 us
  waiting for transfers between devices  198 us (59%)
  blocking collectives  57.7 us (17%)
  matrix products  33.4 us (10%)
  between operations  18.7 us (6%)
  other arithmetic  16.8 us (5%)
  local copies, waits for them, and re-layouts  11 us (3%)
    all_gather x2, waiting for transfers between devices, teacher(): key_block = lax.all_gather(key_rows, 'seq', axis=0, tiled=True)  83.3 us
    all_gather x2, waiting for transfers between devices, teacher(): value_block = lax.all_gather(value_rows, 'seq', axis=0, tiled=True)  49 us
    reduce_scatter x2, waiting for transfers between devices, on_device(): lax.psum_scatter(partial_value.astype(jnp.bfloat16), 'tp', scatter_dimens...  47.8 us
    psum x1, blocking collectives, on_device(): image_sum = lax.psum(image_part, ('seq', 'tp'))  39.3 us
    reduce_scatter x1, waiting for transfers between devices, on_device(): lax.psum_scatter(student_terms.astype(jnp.bfloat16), 'tp', scatter_dimens...  18.1 us
    all_gather x1, blocking collectives, on_device(): whole_rows = lax.all_gather(latents, 'tp', axis=1, tiled=True)  10.4 us
    all_gather x1, blocking collectives, on_device(): whole_rows = lax.all_gather(state_shard, 'tp', axis=1, tiled=True)  8.03 us
    dot_general x2, matrix products, teacher(): jnp.dot(hidden, k_weight, preferred_element_type=jnp.float32)  7.02 us
  transfers between devices with their start and end apart: 7, of which 7 were waited for; matrix products, arithmetic and copies ran while one was open for 11% of the time, Pallas kernels for 0%

commit v1 on v0

--- a/solution.py
+++ b/solution.py
@@ -145,7 +145,7 @@
         student32 * student32, axis=1
     )
     image_part = jnp.sum(one_hot * per_token[:, None], axis=0)
-    image_sum = lax.psum(image_part, ("seq", "tp"))
+    image_sum = lax.psum(lax.psum(image_part, "tp"), "seq")
     loss = jnp.mean(image_sum / (lengths.astype(jnp.float32) * mod_scale.shape[0]))
     return (target, student_velocity, loss)
 

time: 337 us -> 325 us (0.964)
  blocking collectives: 57.7 us -> 45.7 us
    psum x1 -> x2, blocking collectives: 39.3 us -> 27.3 us  [on_device(): image_sum = lax.psum(lax.psum(image_part, 'tp'), 'seq')]
where the time goes in v1:
time: 325 us; the launch traced here: 324 us
  waiting for transfers between devices  198 us (61%)
  blocking collectives  45.7 us (14%)
  matrix products  33.4 us (10%)
  between operations  18.7 us (6%)
  other arithmetic  16.8 us (5%)
  local copies, waits for them, and re-layouts  11 us (3%)
    all_gather x2, waiting for transfers between devices, teacher(): key_block = lax.all_gather(key_rows, 'seq', axis=0, tiled=True)  83.3 us
    all_gather x2, waiting for transfers between devices, teacher(): value_block = lax.all_gather(value_rows, 'seq', axis=0, tiled=True)  49 us
    reduce_scatter x2, waiting for transfers between devices, on_device(): lax.psum_scatter(partial_value.astype(jnp.bfloat16), 'tp', scatter_dimens...  47.8 us
    psum x2, blocking collectives, on_device(): image_sum = lax.psum(lax.psum(image_part, 'tp'), 'seq')  27.3 us
    reduce_scatter x1, waiting for transfers between devices, on_device(): lax.psum_scatter(student_terms.astype(jnp.bfloat16), 'tp', scatter_dimens...  18.1 us
    all_gather x1, blocking collectives, on_device(): whole_rows = lax.all_gather(latents, 'tp', axis=1, tiled=True)  10.4 us
    all_gather x1, blocking collectives, on_device(): whole_rows = lax.all_gather(state_shard, 'tp', axis=1, tiled=True)  8.03 us
    dot_general x2, matrix products, teacher(): jnp.dot(hidden, k_weight, preferred_element_type=jnp.float32)  7.02 us
  transfers between devices with their start and end apart: 7, of which 7 were waited for; matrix products, arithmetic and copies ran while one was open for 11% of the time, Pallas kernels for 0%

profile of v1, /device:TPU:0, one launch (start us, length us, event | category | flops | bytes accessed | tf_op | source)
XLA Modules:
  0.0 324.3 jit_solution(381760950746596017)
XLA Ops:
  8.1 10.4 %all_gather.18 = bf16[128,3072]{1,0:T(8,128)(2,1)S(1)} all-gather(bf16[128,768]{1,0:T(8,128)(2,1)} %param.15), channel_id=1, replica_groups=mesh['seq'=8,'tp'=4] {'tp'}, dimensions={1}, use_global_device_ids=true | all-gather | bytes 983040 | tf_op jit(solution)/shard_map/all_gather | solution.py:105
  23.6 3.1 convolution_convert_fusion.4
  26.8 3.4 %fusion.70 = (f32[128,512]{1,0:T(8,128)}, f32[128,512]{1,0:T(8,128)S(1)}) fusion(bf16[128,3072]{1,0:T(8,128)(2,1)} %copy-done.1, bf16[3072,512]{1,0:T(8,128)(2,1)} %param.20), kind=kOutput, calls=%fused_computation.115 | convolution fusion | flops 402718720 | bytes 4456448 | tf_op jit(solution)/shard_map/dot_general | solution.py:31
  30.2 1.8 mul.218
  38.0 2.7 fusion.72
  42.9 25.1 %all-gather.7.cloned.1.call-done = bf16[1024,512]{1,0:T(8,128)(2,1)} async-done(((bf16[128,512]{1,0:T(8,128)(2,1)}), bf16[1024,512]{1,0:T(8,128)(2,1)}) %all-gather.7.cloned.1.call-update) | async-done | bytes 1048592 | tf_op jit(solution)/shard_map/all_gather | solution.py:67
  68.0 41.7 %all-gather.5.cloned.1.call-done = bf16[1024,512]{1,0:T(8,128)(2,1)} async-done(((bf16[128,512]{1,0:T(8,128)(2,1)}), bf16[1024,512]{1,0:T(8,128)(2,1)}) %all-gather.5.cloned.1.call-update) | async-done | bytes 1048592 | tf_op jit(solution)/shard_map/all_gather | solution.py:66
  109.7 6.0 %conditional.2 = (f32[128,4]{0,1:T(4,128)S(1)}, f32[128,4,128]{0,2,1:T(8,128)S(1)}) conditional(s32[]{:T(128)} %convert_element_type.124, () %tuple.24, (s32[128]{0:T(128)S(1)}, s32[2]{0:T(128)}, bf16[1024,512]{1,0:T(8,128)(2,1)}, bf16[128,4,128]{2,0,1:T(8,128)(2,1)S(1)}, bf16[1024,512]{1,0:T(8,128)(2,1)}) %tuple.59), branch_computations={%region_8.9_spmd, %region_9.13_spmd} | conditional | flops 275386880 | bytes 14045748 | solution.py:72
  110.7 1.7 fusion
  117.4 22.0 %reduce-scatter.4.cloned.1.call-done = bf16[128,768]{1,0:T(8,128)(2,1)} async-done(((bf16[128,3072]{1,0:T(8,128)(2,1)}), bf16[128,768]{1,0:T(8,128)(2,1)}) %reduce-scatter.4.cloned.1.call-update) | async-done | bytes 196624 | tf_op jit(solution)/shard_map/reduce_scatter | solution.py:127
  140.4 8.0 %all_gather.21 = bf16[128,3072]{1,0:T(8,128)(2,1)S(1)} all-gather(bf16[128,768]{1,0:T(8,128)(2,1)S(1)} %fusion.43), channel_id=1, replica_groups=mesh['seq'=8,'tp'=4] {'tp'}, dimensions={1}, use_global_device_ids=true | all-gather | bytes 983040 | tf_op jit(solution)/shard_map/all_gather | solution.py:111
  149.3 3.2 convolution_convert_fusion.3
  152.6 3.6 %fusion.71 = (f32[128,512]{1,0:T(8,128)}, f32[128,512]{1,0:T(8,128)}) fusion(bf16[3072,512]{1,0:T(8,128)(2,1)} %param.20, bf16[128,3072]{1,0:T(8,128)(2,1)} %copy-done.3, f32[128]{0:T(128)S(1)} %broadcast_add_fusion, f32[128]{0:T(128)S(1)} %add_rsqrt_fusion.4, f32[3072]{0:T(1024)S(1)} %copy-done.6), kind=kOutput, calls=%fused_computation.116 | convolution fusion | flops 405078016 | bytes 4469760 | tf_op jit(solution)/shard_map/dot_general | solution.py:31
  159.4 4.2 %convolution_convert_fusion.2 = bf16[128,3072]{1,0:T(8,128)(2,1)} fusion(bf16[768,3072]{1,0:T(8,128)(2,1)} %param.25, bf16[128,3072]{1,0:T(8,128)(2,1)} %copy-done.1, s32[]{:T(128)S(6)} %select_n.16), kind=kOutput, calls=%fused_computation.48 | convolution fusion | flops 604372992 | bytes 5701636 | tf_op jit(solution)/shard_map/dot_general | solution.py:135
  163.7 3.5 %fusion.64 = f32[128,512]{1,0:T(8,128)} fusion(bf16[3072,512]{1,0:T(8,128)(2,1)} %param.19, bf16[128,3072]{1,0:T(8,128)(2,1)} %copy-done.3, f32[128]{0:T(128)S(1)} %broadcast_add_fusion, f32[128]{0:T(128)S(1)} %add_rsqrt_fusion.4, f32[3072]{0:T(1024)S(1)} %copy-done.6), kind=kOutput, calls=%fused_computation.112 | convolution fusion | flops 405012480 | bytes 4207616 | tf_op jit(solution)/shard_map/dot_general | solution.py:30
  169.6 23.9 %all-gather.11.cloned.1.call-done = bf16[1024,512]{1,0:T(8,128)(2,1)} async-done(((bf16[128,512]{1,0:T(8,128)(2,1)}), bf16[1024,512]{1,0:T(8,128)(2,1)}) %all-gather.11.cloned.1.call-update) | async-done | bytes 1048592 | tf_op jit(solution)/shard_map/all_gather | solution.py:67
  193.5 41.6 %all-gather.9.cloned.1.call-done = bf16[1024,512]{1,0:T(8,128)(2,1)} async-done(((bf16[128,512]{1,0:T(8,128)(2,1)}), bf16[1024,512]{1,0:T(8,128)(2,1)}) %all-gather.9.cloned.1.call-update) | async-done | bytes 1048592 | tf_op jit(solution)/shard_map/all_gather | solution.py:66
  235.1 5.3 %conditional.3 = (f32[128,4]{0,1:T(4,128)S(1)}, f32[128,4,128]{0,2,1:T(8,128)S(1)}) conditional(s32[]{:T(128)} %convert_element_type.124, () %tuple.26, (s32[128]{0:T(128)S(1)}, s32[2]{0:T(128)S(1)}, bf16[1024,512]{1,0:T(8,128)(2,1)}, bf16[128,4,128]{2,0,1:T(8,128)(2,1)S(1)}, bf16[1024,512]{1,0:T(8,128)(2,1)}) %tuple.60), branch_computations={%region_17.18_spmd, %region_18.0_spmd} | conditional | flops 275386880 | bytes 14045748 | solution.py:72
  235.4 1.8 fusion.18
  242.0 18.1 %reduce-scatter.8.cloned.1.call-done = bf16[128,768]{1,0:T(8,128)(2,1)} async-done(((bf16[128,3072]{1,0:T(8,128)(2,1)}), bf16[128,768]{1,0:T(8,128)(2,1)}) %reduce-scatter.8.cloned.1.call-update) | async-done | bytes 196624 | tf_op jit(solution)/shard_map/reduce_scatter | solution.py:136
  260.0 25.8 %reduce-scatter.6.cloned.1.call-done = bf16[128,768]{1,0:T(8,128)(2,1)} async-done(((bf16[128,3072]{1,0:T(8,128)(2,1)}), bf16[128,768]{1,0:T(8,128)(2,1)}) %reduce-scatter.6.cloned.1.call-update) | async-done | bytes 196624 | tf_op jit(solution)/shard_map/reduce_scatter | solution.py:127
  285.8 1.8 fusion.48
  287.8 5.8 %psum.14 = f32[2]{0:T(128)S(1)} all-reduce(f32[2]{0:T(128)S(1)} %select_reduce_fusion), channel_id=1, replica_groups=mesh['seq'=8,'tp'=4] {'tp'}, use_global_device_ids=true, to_apply=%region_27.28 | all-reduce | flops 2 | bytes 16 | tf_op jit(solution)/shard_map/psum | solution.py:148
  293.5 21.5 %psum.15 = f32[2]{0:T(128)S(1)} all-reduce(f32[2]{0:T(128)S(1)} %psum.14), channel_id=1, replica_groups=mesh['seq'=8,'tp'=4] {'seq'}, use_global_device_ids=true, to_apply=%region_28.29 | all-reduce | flops 2 | bytes 16 | tf_op jit(solution)/shard_map/psum | solution.py:148
  (99 shorter events, 30.8 us)
Async XLA Ops:
  7.2 108.6 %copy-start = (bf16[512,3072]{1,0:T(8,128)(2,1)S(1)}, bf16[512,3072]{1,0:T(8,128)(2,1)}, u32[]{:S(2)}) copy-start(bf16[512,3072]{1,0:T(8,128)(2,1)} %param.22) | copy-start | bytes 9437188
  7.2 60.8 %all-gather.7.cloned.1.call-start = ((), (), s32[]{:S(2)}) async-start(), calls=%async_computation.4 | async-start | bytes 1179648 | tf_op jit(solution)/shard_map/all_gather | solution.py:67
  18.5 0.9 copy-start.2
  20.4 14.4 %copy-start.8 = (s32[2,1]{0,1:T(1,128)}, s32[2,1]{0,1:T(1,128)S(1)}, u32[]{:S(2)}) copy-start(s32[2,1]{0,1:T(1,128)S(1)} %reduce-window.4) | copy-start | bytes 28
  20.6 0.6 copy-start.10
  22.7 0.9 copy-start.1
  26.7 6.4 %copy-start.12 = (f32[128]{0:T(128)S(1)}, f32[128]{0:T(128)}, u32[]{:S(2)}) copy-start(f32[128]{0:T(128)} %param.24) | copy-start | bytes 1540
  26.7 83.0 %all-gather.5.cloned.1.call-start = ((), (), s32[]{:S(2)}) async-start(), calls=%async_computation.3 | async-start | bytes 1179648 | tf_op jit(solution)/shard_map/all_gather | solution.py:66
  34.1 105.3 %reduce-scatter.4.cloned.1.call-start = ((), (), s32[]{:S(2)}) async-start(), calls=%async_computation.5 | async-start | bytes 983040 | tf_op jit(solution)/shard_map/reduce_scatter | solution.py:127
  38.0 4.8 %copy-start.7 = (f32[128]{0:T(128)S(1)}, f32[128]{0:T(128)}, u32[]{:S(2)}) copy-start(f32[128]{0:T(128)} %param.23) | copy-start | bytes 1540
  109.7 2.8 copy-start.14
  115.8 1.6 copy-start.11
  115.8 23.6 %copy-start.5 = (bf16[128,768]{1,0:T(8,128)(2,1)S(1)}, bf16[128,768]{1,0:T(8,128)(2,1)}, u32[]{:S(2)}) copy-start(bf16[128,768]{1,0:T(8,128)(2,1)} %param.15) | copy-start | bytes 589828
  117.3 32.0 %copy-start.6 = (f32[3072]{0:T(1024)S(1)}, f32[3072]{0:T(1024)}, u32[]{:S(2)}) copy-start(f32[3072]{0:T(1024)} %param.18) | copy-start | bytes 36868
  117.3 76.2 %all-gather.11.cloned.1.call-start = ((), (), s32[]{:S(2)}) async-start(), calls=%async_computation.7 | async-start | bytes 1179648 | tf_op jit(solution)/shard_map/all_gather | solution.py:67
  148.4 0.9 copy-start.3
  152.5 82.5 %all-gather.9.cloned.1.call-start = ((), (), s32[]{:S(2)}) async-start(), calls=%async_computation.6 | async-start | bytes 1179648 | tf_op jit(solution)/shard_map/all_gather | solution.py:66
  159.3 100.7 %reduce-scatter.8.cloned.1.call-start = ((), (), s32[]{:S(2)}) async-start(), calls=%async_computation.9 | async-start | bytes 983040 | tf_op jit(solution)/shard_map/reduce_scatter | solution.py:136
  163.6 122.2 %reduce-scatter.6.cloned.1.call-start = ((), (), s32[]{:S(2)}) async-start(), calls=%async_computation.8 | async-start | bytes 983040 | tf_op jit(solution)/shard_map/reduce_scatter | solution.py:127
  163.7 71.4 %copy-start.9 = (s32[2,1]{0,1:T(1,128)S(1)}, s32[2,1]{0,1:T(1,128)}, u32[]{:S(2)}) copy-start(s32[2,1]{0,1:T(1,128)} %copy-done.8) | copy-start | bytes 28
  235.1 2.1 copy-start.13
  240.4 45.4 %copy-start.4 = (bf16[128,768]{1,0:T(8,128)(2,1)S(1)}, bf16[128,768]{1,0:T(8,128)(2,1)}, u32[]{:S(2)}) copy-start(bf16[128,768]{1,0:T(8,128)(2,1)} %reduce-scatter.4.cloned.1.call-done) | copy-start | bytes 589828
  240.4 74.6 %copy-start.15 = (s32[2]{0:T(128)S(1)}, s32[2]{0:T(128)}, u32[]{:S(2)}) copy-start(s32[2]{0:T(128)} %param.16) | copy-start | bytes 28
Sparse Core Ops, SparseCore 0:
  26.8 41.1 all-gather.6
  70.7 38.9 all-gather.4
  117.4 21.9 reduce-scatter.3
  152.6 40.8 all-gather.10
  196.0 38.9 all-gather.8
  238.0 21.9 reduce-scatter.7
  262.5 23.2 reduce-scatter.5
